TPU v7x, 32 devices: a whole 2x2x4 slice. The times are simulated.
32 devices in a mesh: row: 4 (over y, x), col: 8 (over z, core).
Axes of the slice: x: 2, y: 2, z: 4, core: 2. Of those that a mesh axis runs over, the one named last changes fastest.
Arguments:
- hidden_states: bfloat16 [1536, 4096], P('col', 'row'), may hold values from -50 to 50
- out_grad: bfloat16 [1536, 4096], P('col', 'row'), may hold values from -6 to 6
- lengths: int32 [4, 4], P('row'), may hold values from 1 to 512, 1024 in all within a row
- norm_gains: bfloat16 [2, 2, 1536], P(None, None, 'col'), may hold values from 0.099609375 to 1.8984375
- qkv_weight: bfloat16 [2, 1536, 2048], P(None, 'row', 'col'), may hold values from -0.15625 to 0.15625
- qkv_bias: bfloat16 [2, 16, 128], P(None, 'col', 'row'), may hold values from -2 to 2
- out_weight: bfloat16 [2, 1536, 1536], P(None, 'col', 'row'), may hold values from -0.625 to 0.625
- gate_weight: bfloat16 [2, 1536, 8960], P(None, 'row', 'col'), may hold values from -0.15625 to 0.15625
- up_weight: bfloat16 [2, 1536, 8960], P(None, 'row', 'col'), may hold values from -0.15625 to 0.15625
- down_weight: bfloat16 [2, 8960, 1536], P(None, 'col', 'row'), may hold values from -0.0625 to 0.0625
Outputs:
- out_states: bfloat16 [1536, 4096], P('col', 'row')
- input_grad: float32 [1536, 4096], P('col', 'row')
- norm_gains_grad: float32 [2, 2, 1536], P(None, None, 'col')
- qkv_weight_grad: float32 [2, 1536, 2048], P(None, 'row', 'col')
- qkv_bias_grad: float32 [2, 16, 128], P(None, 'col', 'row')
- out_weight_grad: float32 [2, 1536, 1536], P(None, 'col', 'row')
- gate_weight_grad: float32 [2, 1536, 8960], P(None, 'row', 'col')
- up_weight_grad: float32 [2, 1536, 8960], P(None, 'row', 'col')
- down_weight_grad: float32 [2, 8960, 1536], P(None, 'col', 'row')
Inputs may be any that keep to these rules, and one draw needn't show every extreme that they name: Row g lists, in order, the lengths of the sequences packed into row group g; each row sums to 1024 and holds one length of exactly 512.
All inputs are finite; a program needn't handle non-finite values.
Results may differ from a plain program's by a relative error of at most 0.017.
Values may be sent and summed in bfloat16 or wider, within the bound.
A program may use at most 256 MiB of HBM per device.

v0:
```python
from functools import partial
import jax
import jax.numpy as jnp
from jax import lax
from jax.sharding import PartitionSpec as P

D = 1536
HEADS = 12
KV_HEADS = 2
HD = 128
LAYERS = 2
SEQ_MAX = 512
QB = 128
eps_norm = 1e-06
rope_base = 1000000.0
neg_fill = -1e30


def row_starts(sizes, count):
    ends = jnp.cumsum(sizes)
    firsts = ends - sizes
    places = jnp.arange(count, dtype=jnp.int32)
    inside = (places[None, :] >= firsts[:, None]) & (places[None, :] < ends[:, None])
    return jnp.sum(jnp.where(inside, firsts[:, None], 0), axis=0)


def rope_tables(positions):
    half = HD // 2
    freq = rope_base ** (-(jnp.arange(half, dtype=jnp.float32) * (2.0 / HD)))
    angle = freq[:, None] * positions.astype(jnp.float32)[None, :]
    cosine = jnp.concatenate([jnp.cos(angle), jnp.cos(angle)], axis=0)
    sine = jnp.concatenate([jnp.sin(angle), jnp.sin(angle)], axis=0)
    return (cosine, sine)


def rotate(values, cosine, sine):
    half = HD // 2
    turned = jnp.concatenate([-values[:, half:], values[:, :half]], axis=1)
    return values * cosine + turned * sine


def rotate_back(grads, cosine, sine):
    half = HD // 2
    lifted = grads * sine
    turned = jnp.concatenate([lifted[:, half:], -lifted[:, :half]], axis=1)
    return grads * cosine + turned


def contract_first(left, right):
    return lax.dot_general(
        left, right, (((0,), (0,)), ((), ())), preferred_element_type=jnp.float32
    )


def contract_last(left, right):
    return lax.dot_general(
        left, right, (((1,), (1,)), ((), ())), preferred_element_type=jnp.float32
    )


def feature_total(values):
    return lax.psum(jnp.sum(values, axis=0), "col")


def spread(values):
    return lax.all_gather(values, "col", axis=0, tiled=True)


def summed_rows(make_term, rows):
    return lax.psum_scatter(
        make_term(jnp.int32(0), lax.axis_size("col") * rows), "col", scatter_dimension=0, tiled=True
    )


def to_blocks(values):
    return lax.all_to_all(values, "col", split_axis=1, concat_axis=0, tiled=True)


def to_tokens(values):
    return lax.all_to_all(values, "col", split_axis=0, concat_axis=1, tiled=True)


def by_columns(weight, acts, start, count):
    return contract_first(weight, acts)


def by_rows(weight, grads, start, count):
    return jnp.dot(weight, grads, preferred_element_type=jnp.float32)


def by_rows_pair(first_weight, first_grads, second_weight, second_grads, start, count):
    return by_rows(first_weight, first_grads, start, count) + by_rows(
        second_weight, second_grads, start, count
    )


def norm_forward(residual, gain):
    totals = feature_total(residual * residual)
    scale = lax.rsqrt(totals / D + eps_norm)
    return (scale, (residual * scale * gain[:, None]).astype(jnp.bfloat16))


def norm_backward(d_normed, residual, scale, gain):
    weighted = d_normed * gain[:, None]
    inner = feature_total(weighted * residual)
    d_residual = weighted * scale - residual * (scale * scale * scale) * inner / D
    d_gain = jnp.sum(d_normed * residual * scale, axis=1)
    return (d_residual, d_gain)


def attend_scores(queries, keys, mask):
    scores = jnp.einsum(
        "kghq,khj->kgqj", queries, keys, preferred_element_type=jnp.float32
    ) * HD ** (-0.5)
    return jnp.where(mask[None, None], scores, neg_fill)


def per_device(
    hidden_states,
    out_grad,
    lengths,
    norm_gains,
    qkv_weight,
    qkv_bias,
    out_weight,
    gate_weight,
    up_weight,
    down_weight,
):
    feat_rows, tok_row = hidden_states.shape
    col_at = lax.axis_index("col")
    starts = row_starts(lengths[0], tok_row)
    positions = jnp.arange(tok_row, dtype=jnp.int32) - starts
    cosine, sine = rope_tables(positions)
    first = col_at * QB
    block_starts = lax.dynamic_slice_in_dim(starts, first, QB)
    cos_block = lax.dynamic_slice_in_dim(cosine, first, QB, 1)
    sin_block = lax.dynamic_slice_in_dim(sine, first, QB, 1)
    reach = QB + SEQ_MAX
    window = jnp.maximum(first - SEQ_MAX, 0)
    key_places = window + jnp.arange(reach, dtype=jnp.int32)
    query_places = first + jnp.arange(QB, dtype=jnp.int32)
    mask = (key_places[None, :] >= block_starts[:, None]) & (
        key_places[None, :] <= query_places[:, None]
    )
    group = HEADS // KV_HEADS
    rotary = HEADS + KV_HEADS
    query_rows = HEADS * HD
    kv_rows = KV_HEADS * HD
    gains = norm_gains.astype(jnp.float32)
    residual = hidden_states.astype(jnp.float32)
    saved = []
    for layer in range(LAYERS):
        w_qkv, b_qkv, w_out, w_gate, w_up, w_down = (
            lax.all_gather(qkv_weight[layer], "row", axis=0, tiled=True),
            lax.all_gather(qkv_bias[layer], "row", axis=1, tiled=True),
            lax.all_gather(out_weight[layer], "row", axis=1, tiled=True),
            lax.all_gather(gate_weight[layer], "row", axis=0, tiled=True),
            lax.all_gather(up_weight[layer], "row", axis=0, tiled=True),
            lax.all_gather(down_weight[layer], "row", axis=1, tiled=True),
        )
        scale_one, normed_one = norm_forward(residual, gains[layer, 0])
        full_one = spread(normed_one)
        raw = contract_first(w_qkv, full_one) + b_qkv.reshape(-1).astype(jnp.float32)[:, None]
        local_heads = raw.shape[0] // HD
        shaped = raw.reshape(local_heads, HD, tok_row)
        head_ids = col_at * local_heads + jnp.arange(local_heads)
        turned = jnp.where((head_ids < rotary)[:, None, None], rotate(shaped, cosine, sine), shaped)
        blocked = to_blocks(turned.reshape(raw.shape).astype(jnp.bfloat16))
        kv_full = lax.all_gather(blocked[query_rows:], "col", axis=1, tiled=True)
        kv_window = lax.dynamic_slice_in_dim(kv_full, window, reach, 1)
        queries = blocked[:query_rows].reshape(KV_HEADS, group, HD, QB)
        keys = kv_window[:kv_rows].reshape(KV_HEADS, HD, reach)
        values = kv_window[kv_rows:].reshape(KV_HEADS, HD, reach)
        masked = attend_scores(queries, keys, mask)
        row_top = jnp.max(masked, axis=-1, keepdims=True)
        lifted = jnp.exp(masked - row_top)
        row_mass = jnp.sum(lifted, axis=-1, keepdims=True)
        probs = lifted / row_mass
        log_mass = row_top + jnp.log(row_mass)
        mixed = (
            jnp.einsum(
                "kgqj,khj->kghq",
                probs.astype(jnp.bfloat16),
                values,
                preferred_element_type=jnp.float32,
            )
            .reshape(query_rows, QB)
            .astype(jnp.bfloat16)
        )
        carried = to_tokens(mixed)
        attention = summed_rows(partial(by_columns, w_out, carried), feat_rows)
        residual_mid = residual + attention
        scale_two, normed_two = norm_forward(residual_mid, gains[layer, 1])
        full_two = spread(normed_two)
        gate = contract_first(w_gate, full_two)
        up = contract_first(w_up, full_two)
        hidden = (gate * jax.nn.sigmoid(gate) * up).astype(jnp.bfloat16)
        feed = summed_rows(partial(by_columns, w_down, hidden), feat_rows)
        saved.append(
            (
                residual,
                scale_one,
                full_one,
                blocked,
                kv_window,
                log_mass,
                mixed,
                carried,
                residual_mid,
                scale_two,
                full_two,
                gate,
                up,
                hidden,
                (w_qkv, w_out, w_gate, w_up, w_down),
                local_heads,
            )
        )
        residual = residual_mid + feed
    out_states = residual.astype(jnp.bfloat16)
    grad = out_grad.astype(jnp.float32)
    layer_grads = [None] * LAYERS
    gain_terms = [None] * LAYERS
    for layer in reversed(range(LAYERS)):
        (
            residual_in,
            scale_one,
            full_one,
            blocked,
            kv_window,
            log_mass,
            mixed,
            carried,
            residual_mid,
            scale_two,
            full_two,
            gate,
            up,
            hidden,
            weights_full,
            local_heads,
        ) = saved[layer]
        w_qkv, w_out, w_gate, w_up, w_down = weights_full
        grad_full = spread(grad.astype(jnp.bfloat16))
        d_down = contract_last(hidden, grad_full)
        d_hidden = jnp.dot(w_down, grad_full, preferred_element_type=jnp.float32)
        squash = jax.nn.sigmoid(gate)
        d_gate = (d_hidden * up * squash * (1.0 + gate * (1.0 - squash))).astype(jnp.bfloat16)
        d_up = (d_hidden * gate * squash).astype(jnp.bfloat16)
        d_gate_w = contract_last(full_two, d_gate)
        d_up_w = contract_last(full_two, d_up)
        d_normed_two = summed_rows(partial(by_rows_pair, w_gate, d_gate, w_up, d_up), feat_rows)
        d_residual, d_gain_two = norm_backward(
            d_normed_two, residual_mid, scale_two, gains[layer, 1]
        )
        grad = grad + d_residual
        grad_full = spread(grad.astype(jnp.bfloat16))
        d_out_w = contract_last(carried, grad_full)
        d_mixed = to_blocks(
            jnp.dot(w_out, grad_full, preferred_element_type=jnp.float32).astype(jnp.bfloat16)
        )
        queries = blocked[:query_rows].reshape(KV_HEADS, group, HD, QB)
        keys = kv_window[:kv_rows].reshape(KV_HEADS, HD, reach)
        values = kv_window[kv_rows:].reshape(KV_HEADS, HD, reach)
        masked = attend_scores(queries, keys, mask)
        probs = jnp.exp(masked - log_mass)
        low_probs = probs.astype(jnp.bfloat16)
        d_heads_mix = d_mixed.reshape(KV_HEADS, group, HD, QB)
        d_probs = jnp.einsum(
            "kghq,khj->kgqj", d_heads_mix, values, preferred_element_type=jnp.float32
        )
        inner = jnp.sum(probs * d_probs, axis=-1, keepdims=True)
        d_scores = (probs * (d_probs - inner)).astype(jnp.bfloat16)
        d_queries = (
            jnp.einsum("kgqj,khj->kghq", d_scores, keys, preferred_element_type=jnp.float32)
            * HD ** (-0.5)
        ).reshape(query_rows, QB)
        d_keys = (
            jnp.einsum("kgqj,kghq->khj", d_scores, queries, preferred_element_type=jnp.float32)
            * HD ** (-0.5)
        ).reshape(kv_rows, reach)
        d_values = jnp.einsum(
            "kgqj,kghq->khj", low_probs, d_heads_mix, preferred_element_type=jnp.float32
        ).reshape(kv_rows, reach)
        d_window = jnp.concatenate([d_keys, d_values], axis=0)
        d_placed = lax.dynamic_update_slice_in_dim(
            jnp.zeros((2 * kv_rows, tok_row), jnp.float32), d_window, window, 1
        )
        d_kv = lax.psum_scatter(d_placed, "col", scatter_dimension=1, tiled=True)
        d_heads = jnp.concatenate([d_queries, d_kv], axis=0).reshape(HEADS + 2 * KV_HEADS, HD, QB)
        d_turned = jnp.concatenate(
            [rotate_back(d_heads[:rotary], cos_block, sin_block), d_heads[rotary:]], axis=0
        )
        d_raw = to_tokens(d_turned.reshape((HEADS + 2 * KV_HEADS) * HD, QB).astype(jnp.bfloat16))
        d_bias = jnp.sum(d_raw, axis=1, dtype=jnp.float32).reshape(local_heads, HD)
        d_qkv_w = contract_last(full_one, d_raw)
        d_normed_one = summed_rows(partial(by_rows, w_qkv, d_raw), feat_rows)
        d_residual, d_gain_one = norm_backward(
            d_normed_one, residual_in, scale_one, gains[layer, 0]
        )
        grad = grad + d_residual
        layer_grads[layer] = (
            lax.psum_scatter(d_qkv_w, "row", scatter_dimension=0, tiled=True),
            lax.psum_scatter(d_bias, "row", scatter_dimension=1, tiled=True),
            lax.psum_scatter(d_out_w, "row", scatter_dimension=1, tiled=True),
            lax.psum_scatter(d_gate_w, "row", scatter_dimension=0, tiled=True),
            lax.psum_scatter(d_up_w, "row", scatter_dimension=0, tiled=True),
            lax.psum_scatter(d_down, "row", scatter_dimension=1, tiled=True),
        )
        gain_terms[layer] = jnp.stack([d_gain_one, d_gain_two])
    gain_grads = lax.psum(jnp.stack(gain_terms), "row")
    stacked = [jnp.stack([entry[member] for entry in layer_grads]) for member in range(6)]
    return (
        out_states,
        grad,
        gain_grads,
        stacked[0],
        stacked[1],
        stacked[2],
        stacked[3],
        stacked[4],
        stacked[5],
    )


def solution(mesh):
    placed = (
        P("col", "row"),
        P("col", "row"),
        P("row", None),
        P(None, None, "col"),
        P(None, "row", "col"),
        P(None, "col", "row"),
        P(None, "col", "row"),
        P(None, "row", "col"),
        P(None, "row", "col"),
        P(None, "col", "row"),
    )
    return jax.shard_map(
        per_device,
        mesh=mesh,
        in_specs=placed,
        out_specs=(
            P("col", "row"),
            P("col", "row"),
            P(None, None, "col"),
            P(None, "row", "col"),
            P(None, "col", "row"),
            P(None, "col", "row"),
            P(None, "row", "col"),
            P(None, "row", "col"),
            P(None, "col", "row"),
        ),
        check_vma=False,
    )
```

profile of v0, /device:TPU:0, one launch (start us, length us, event | category | flops | bytes accessed | tf_op | source)
XLA Modules:
  0.0 2292.5 jit_solution(13109288929776706779)
XLA Ops:
  153.3 66.9 %reduce-scatter.67.cloned.1.call-done = f32[192,1024]{1,0:T(8,128)} async-done(((f32[1536,1024]{1,0:T(8,128)}), f32[192,1024]{1,0:T(8,128)}) %reduce-scatter.67.cloned.1.call-update) | async-done | bytes 786448 | tf_op jit(solution)/shard_map/reduce_scatter | solution.py:70
  241.1 32.1 %all-gather.33.cloned.1.call-done = bf16[1536,1024]{1,0:T(8,128)(2,1)} async-done(((bf16[192,1024]{1,0:T(8,128)(2,1)}), bf16[1536,1024]{1,0:T(8,128)(2,1)}) %all-gather.33.cloned.1.call-update) | async-done | bytes 3145744 | tf_op jit(solution)/shard_map/all_gather | solution.py:66
  282.0 38.5 %all-gather.51.cloned.1.call-done = bf16[1,1536,1120]{1,2,0:T(8,128)(2,1)} async-done(((bf16[1,384,1120]{1,2,0:T(8,128)(2,1)}), bf16[1,1536,1120]{1,2,0:T(8,128)(2,1)}) %all-gather.51.cloned.1.call-update) | async-done | bytes 3440656 | tf_op jit(solution)/shard_map/all_gather | solution.py:159
  331.7 36.8 %all-gather.53.cloned.1.call-done = bf16[1,1120,1536]{2,1,0:T(8,128)(2,1)} async-done(((bf16[1,1120,384]{2,1,0:T(8,128)(2,1)}), bf16[1,1120,1536]{2,1,0:T(8,128)(2,1)}) %all-gather.53.cloned.1.call-update) | async-done | bytes 3440656 | tf_op jit(solution)/shard_map/all_gather | solution.py:160
  384.8 69.8 %reduce-scatter.69.cloned.1.call-done = f32[192,1024]{1,0:T(8,128)} async-done(((f32[1536,1024]{1,0:T(8,128)}), f32[192,1024]{1,0:T(8,128)}) %reduce-scatter.69.cloned.1.call-update) | async-done | bytes 786448 | tf_op jit(solution)/shard_map/reduce_scatter | solution.py:70
  534.7 22.8 all-gather.37.cloned.1.call-done
  590.3 68.1 %reduce-scatter.71.cloned.1.call-done = f32[192,1024]{1,0:T(8,128)} async-done(((f32[1536,1024]{1,0:T(8,128)}), f32[192,1024]{1,0:T(8,128)}) %reduce-scatter.71.cloned.1.call-update) | async-done | bytes 786448 | tf_op jit(solution)/shard_map/reduce_scatter | solution.py:70
  676.8 27.9 %all-gather.57.cloned.1.call-done = bf16[1,1536,1120]{1,2,0:T(8,128)(2,1)} async-done(((bf16[1,384,1120]{1,2,0:T(8,128)(2,1)}), bf16[1,1536,1120]{1,2,0:T(8,128)(2,1)}) %all-gather.57.cloned.1.call-update) | async-done | bytes 3440656 | tf_op jit(solution)/shard_map/all_gather | solution.py:159
  704.7 40.1 %all-gather.39.cloned.1.call-done = bf16[1536,1024]{1,0:T(8,128)(2,1)} async-done(((bf16[192,1024]{1,0:T(8,128)(2,1)}), bf16[1536,1024]{1,0:T(8,128)(2,1)}) %all-gather.39.cloned.1.call-update) | async-done | bytes 3145744 | tf_op jit(solution)/shard_map/all_gather | solution.py:66
  753.6 38.1 %all-gather.55.cloned.1.call-done = bf16[1,1536,1120]{1,2,0:T(8,128)(2,1)} async-done(((bf16[1,384,1120]{1,2,0:T(8,128)(2,1)}), bf16[1,1536,1120]{1,2,0:T(8,128)(2,1)}) %all-gather.55.cloned.1.call-update) | async-done | bytes 3440656 | tf_op jit(solution)/shard_map/all_gather | solution.py:158
  800.5 38.9 %all-gather.59.cloned.1.call-done = bf16[1,1120,1536]{2,1,0:T(8,128)(2,1)} async-done(((bf16[1,1120,384]{2,1,0:T(8,128)(2,1)}), bf16[1,1120,1536]{2,1,0:T(8,128)(2,1)}) %all-gather.59.cloned.1.call-update) | async-done | bytes 3440656 | tf_op jit(solution)/shard_map/all_gather | solution.py:160
  839.4 39.7 %all-gather.41.cloned.1.call-done = bf16[1536,1024]{1,0:T(8,128)(2,1)} async-done(((bf16[192,1024]{1,0:T(8,128)(2,1)}), bf16[1536,1024]{1,0:T(8,128)(2,1)}) %all-gather.41.cloned.1.call-update) | async-done | bytes 3145744 | tf_op jit(solution)/shard_map/all_gather | solution.py:66
  909.3 68.8 %reduce-scatter.75.cloned.1.call-done = f32[192,1024]{1,0:T(8,128)} async-done(((f32[1536,1024]{1,0:T(8,128)}), f32[192,1024]{1,0:T(8,128)}) %reduce-scatter.75.cloned.1.call-update) | async-done | bytes 786448 | tf_op jit(solution)/shard_map/reduce_scatter | solution.py:70
  995.8 36.7 %all-gather.43.cloned.1.call-done = bf16[1536,1024]{1,0:T(8,128)(2,1)} async-done(((bf16[192,1024]{1,0:T(8,128)(2,1)}), bf16[1536,1024]{1,0:T(8,128)(2,1)}) %all-gather.43.cloned.1.call-update) | async-done | bytes 3145744 | tf_op jit(solution)/shard_map/all_gather | solution.py:66
  1072.1 30.5 %reduce-scatter.43.cloned.1.call-done = f32[512,128]{1,0:T(8,128)} async-done(((f32[512,1024]{1,0:T(8,128)}), f32[512,128]{1,0:T(8,128)}) %reduce-scatter.43.cloned.1.call-update) | async-done | bytes 262160 | tf_op jit(solution)/shard_map/reduce_scatter | solution.py:290
  1150.8 52.5 %reduce-scatter.77.cloned.1.call-done = f32[192,1024]{1,0:T(8,128)} async-done(((f32[1536,1024]{1,0:T(8,128)}), f32[192,1024]{1,0:T(8,128)}) %reduce-scatter.77.cloned.1.call-update) | async-done | bytes 786448 | tf_op jit(solution)/shard_map/reduce_scatter | solution.py:70
  1219.9 54.1 %reduce-scatter.73.cloned.1.call-done = f32[192,1024]{1,0:T(8,128)} async-done(((f32[1536,1024]{1,0:T(8,128)}), f32[192,1024]{1,0:T(8,128)}) %reduce-scatter.73.cloned.1.call-update) | async-done | bytes 786448 | tf_op jit(solution)/shard_map/reduce_scatter | solution.py:70
  1277.1 36.1 %all-gather.45.cloned.1.call-done = bf16[1536,1024]{1,0:T(8,128)(2,1)} async-done(((bf16[192,1024]{1,0:T(8,128)(2,1)}), bf16[1536,1024]{1,0:T(8,128)(2,1)}) %all-gather.45.cloned.1.call-update) | async-done | bytes 3145744 | tf_op jit(solution)/shard_map/all_gather | solution.py:66
  1341.7 68.6 %reduce-scatter.79.cloned.1.call-done = f32[192,1024]{1,0:T(8,128)} async-done(((f32[1536,1024]{1,0:T(8,128)}), f32[192,1024]{1,0:T(8,128)}) %reduce-scatter.79.cloned.1.call-update) | async-done | bytes 786448 | tf_op jit(solution)/shard_map/reduce_scatter | solution.py:70
  1427.8 36.7 %all-gather.47.cloned.1.call-done = bf16[1536,1024]{1,0:T(8,128)(2,1)} async-done(((bf16[192,1024]{1,0:T(8,128)(2,1)}), bf16[1536,1024]{1,0:T(8,128)(2,1)}) %all-gather.47.cloned.1.call-update) | async-done | bytes 3145744 | tf_op jit(solution)/shard_map/all_gather | solution.py:66
  1607.8 29.6 %reduce-scatter.65.cloned.1.call-done = f32[1120,384]{1,0:T(8,128)} async-done(((f32[1120,1536]{1,0:T(8,128)}), f32[1120,384]{1,0:T(8,128)}) %reduce-scatter.65.cloned.1.call-update) | async-done | bytes 1720336 | tf_op jit(solution)/shard_map/reduce_scatter | solution.py:309
  1637.4 77.8 %reduce-scatter.63.cloned.1.call-done = f32[1120,384]{1,0:T(8,128)} async-done(((f32[1120,1536]{1,0:T(8,128)}), f32[1120,384]{1,0:T(8,128)}) %reduce-scatter.63.cloned.1.call-update) | async-done | bytes 1720336 | tf_op jit(solution)/shard_map/reduce_scatter | solution.py:309
  1719.2 73.9 %reduce-scatter.61.cloned.1.call-done = f32[384,1120]{0,1:T(8,128)} async-done(((f32[1536,1120]{0,1:T(8,128)}), f32[384,1120]{0,1:T(8,128)}) %reduce-scatter.61.cloned.1.call-update) | async-done | bytes 1720336 | tf_op jit(solution)/shard_map/reduce_scatter | solution.py:308
  1793.1 77.8 %reduce-scatter.59.cloned.1.call-done = f32[384,1120]{0,1:T(8,128)} async-done(((f32[1536,1120]{0,1:T(8,128)}), f32[384,1120]{0,1:T(8,128)}) %reduce-scatter.59.cloned.1.call-update) | async-done | bytes 1720336 | tf_op jit(solution)/shard_map/reduce_scatter | solution.py:308
  1874.9 73.9 %reduce-scatter.57.cloned.1.call-done = f32[384,1120]{0,1:T(8,128)} async-done(((f32[1536,1120]{0,1:T(8,128)}), f32[384,1120]{0,1:T(8,128)}) %reduce-scatter.57.cloned.1.call-update) | async-done | bytes 1720336 | tf_op jit(solution)/shard_map/reduce_scatter | solution.py:307
  1948.7 77.8 %reduce-scatter.55.cloned.1.call-done = f32[384,1120]{0,1:T(8,128)} async-done(((f32[1536,1120]{0,1:T(8,128)}), f32[384,1120]{0,1:T(8,128)}) %reduce-scatter.55.cloned.1.call-update) | async-done | bytes 1720336 | tf_op jit(solution)/shard_map/reduce_scatter | solution.py:307
  2030.5 27.6 %reduce-scatter.53.cloned.1.call-done = f32[192,384]{1,0:T(8,128)} async-done(((f32[192,1536]{1,0:T(8,128)}), f32[192,384]{1,0:T(8,128)}) %reduce-scatter.53.cloned.1.call-update) | async-done | bytes 294928 | tf_op jit(solution)/shard_map/reduce_scatter | solution.py:306
  2058.2 31.5 %reduce-scatter.51.cloned.1.call-done = f32[192,384]{1,0:T(8,128)} async-done(((f32[192,1536]{1,0:T(8,128)}), f32[192,384]{1,0:T(8,128)}) %reduce-scatter.51.cloned.1.call-update) | async-done | bytes 294928 | tf_op jit(solution)/shard_map/reduce_scatter | solution.py:306
  2091.6 24.9 %reduce-scatter.83.cloned.1.call-done = f32[32,2]{1,0:T(8,128)} async-done(((f32[128,2]{1,0:T(8,128)}), f32[32,2]{1,0:T(8,128)}) %reduce-scatter.83.cloned.1.call-update) | async-done | bytes 272
  2117.9 32.8 %reduce-scatter.49.cloned.1.call-done = f32[384,256]{1,0:T(8,128)} async-done(((f32[1536,256]{1,0:T(8,128)}), f32[384,256]{1,0:T(8,128)}) %reduce-scatter.49.cloned.1.call-update) | async-done | bytes 393232 | tf_op jit(solution)/shard_map/reduce_scatter | solution.py:304
  2150.7 34.2 %reduce-scatter.47.cloned.1.call-done = f32[384,256]{1,0:T(8,128)} async-done(((f32[1536,256]{1,0:T(8,128)}), f32[384,256]{1,0:T(8,128)}) %reduce-scatter.47.cloned.1.call-update) | async-done | bytes 393232 | tf_op jit(solution)/shard_map/reduce_scatter | solution.py:304
  2186.9 69.9 %reduce-scatter.81.cloned.1.call-done = f32[192,1024]{1,0:T(8,128)} async-done(((f32[1536,1024]{1,0:T(8,128)}), f32[192,1024]{1,0:T(8,128)}) %reduce-scatter.81.cloned.1.call-update) | async-done | bytes 786448 | tf_op jit(solution)/shard_map/reduce_scatter | solution.py:70
  (426 shorter events, 739.3 us)
Async XLA Ops:
  127.2 92.9 %reduce-scatter.67.cloned.1.call-start = ((), (), s32[]{:S(2)}) async-start(), calls=%async_computation.58 | async-start | bytes 7077888 | tf_op jit(solution)/shard_map/reduce_scatter | solution.py:70
  153.2 120.0 %all-gather.33.cloned.1.call-start = ((), (), s32[]{:S(2)}) async-start(), calls=%async_computation.32 | async-start | bytes 3538944 | tf_op jit(solution)/shard_map/all_gather | solution.py:66
  239.6 128.8 %all-gather.53.cloned.1.call-start = ((), (), s32[]{:S(2)}) async-start(), calls=%async_computation.54 | async-start | bytes 4300800 | tf_op jit(solution)/shard_map/all_gather | solution.py:160
  241.1 213.5 %reduce-scatter.69.cloned.1.call-start = ((), (), s32[]{:S(2)}) async-start(), calls=%async_computation.59 | async-start | bytes 7077888 | tf_op jit(solution)/shard_map/reduce_scatter | solution.py:70
  384.7 122.8 %all-gather.35.cloned.1.call-start = ((), (), s32[]{:S(2)}) async-start(), calls=%async_computation.33 | async-start | bytes 3538944 | tf_op jit(solution)/shard_map/all_gather | solution.py:66
  566.7 91.7 %reduce-scatter.71.cloned.1.call-start = ((), (), s32[]{:S(2)}) async-start(), calls=%async_computation.60 | async-start | bytes 7077888 | tf_op jit(solution)/shard_map/reduce_scatter | solution.py:70
  589.6 115.0 %all-gather.57.cloned.1.call-start = ((), (), s32[]{:S(2)}) async-start(), calls=%async_computation.56 | async-start | bytes 4300800 | tf_op jit(solution)/shard_map/all_gather | solution.py:159
  590.2 154.6 %all-gather.39.cloned.1.call-start = ((), (), s32[]{:S(2)}) async-start(), calls=%async_computation.35 | async-start | bytes 3538944 | tf_op jit(solution)/shard_map/all_gather | solution.py:66
  674.3 117.4 %all-gather.55.cloned.1.call-start = ((), (), s32[]{:S(2)}) async-start(), calls=%async_computation.55 | async-start | bytes 4300800 | tf_op jit(solution)/shard_map/all_gather | solution.py:158
  675.0 164.4 %all-gather.59.cloned.1.call-start = ((), (), s32[]{:S(2)}) async-start(), calls=%async_computation.57 | async-start | bytes 4300800 | tf_op jit(solution)/shard_map/all_gather | solution.py:160
  675.6 203.6 %all-gather.41.cloned.1.call-start = ((), (), s32[]{:S(2)}) async-start(), calls=%async_computation.36 | async-start | bytes 3538944 | tf_op jit(solution)/shard_map/all_gather | solution.py:66
  676.3 301.8 %reduce-scatter.75.cloned.1.call-start = ((), (), s32[]{:S(2)}) async-start(), calls=%async_computation.62 | async-start | bytes 7077888 | tf_op jit(solution)/shard_map/reduce_scatter | solution.py:70
  909.3 123.3 %all-gather.43.cloned.1.call-start = ((), (), s32[]{:S(2)}) async-start(), calls=%async_computation.37 | async-start | bytes 3538944 | tf_op jit(solution)/shard_map/all_gather | solution.py:66
  1067.9 135.4 %reduce-scatter.77.cloned.1.call-start = ((), (), s32[]{:S(2)}) async-start(), calls=%async_computation.63 | async-start | bytes 7077888 | tf_op jit(solution)/shard_map/reduce_scatter | solution.py:70
  1134.4 139.6 %reduce-scatter.73.cloned.1.call-start = ((), (), s32[]{:S(2)}) async-start(), calls=%async_computation.61 | async-start | bytes 7077888 | tf_op jit(solution)/shard_map/reduce_scatter | solution.py:70
  1150.7 162.6 %all-gather.45.cloned.1.call-start = ((), (), s32[]{:S(2)}) async-start(), calls=%async_computation.39 | async-start | bytes 3538944 | tf_op jit(solution)/shard_map/all_gather | solution.py:66
  1276.7 133.6 %reduce-scatter.79.cloned.1.call-start = ((), (), s32[]{:S(2)}) async-start(), calls=%async_computation.64 | async-start | bytes 7077888 | tf_op jit(solution)/shard_map/reduce_scatter | solution.py:70
  1341.6 122.8 %all-gather.47.cloned.1.call-start = ((), (), s32[]{:S(2)}) async-start(), calls=%async_computation.40 | async-start | bytes 3538944 | tf_op jit(solution)/shard_map/all_gather | solution.py:66
  1471.6 95.5 %reduce-scatter.45.cloned.1.call-start = ((), (), s32[]{:S(2)}) async-start(), calls=%async_computation.41 | async-start | bytes 2359296 | tf_op jit(solution)/shard_map/reduce_scatter | solution.py:290
  1498.6 108.4 %reduce-scatter.85.cloned.1.call-start = ((), (), s32[]{:S(2)}) async-start(), calls=%async_computation.67 | async-start | bytes 81920
  1500.6 136.8 %reduce-scatter.65.cloned.1.call-start = ((), (), s32[]{:S(2)}) async-start(), calls=%async_computation.51 | async-start | bytes 8601600 | tf_op jit(solution)/shard_map/reduce_scatter | solution.py:309
  1509.8 205.4 %reduce-scatter.63.cloned.1.call-start = ((), (), s32[]{:S(2)}) async-start(), calls=%async_computation.50 | async-start | bytes 8601600 | tf_op jit(solution)/shard_map/reduce_scatter | solution.py:309
  1519.1 273.9 %reduce-scatter.61.cloned.1.call-start = ((), (), s32[]{:S(2)}) async-start(), calls=%async_computation.49 | async-start | bytes 8601600 | tf_op jit(solution)/shard_map/reduce_scatter | solution.py:308
  1528.7 342.1 %reduce-scatter.59.cloned.1.call-start = ((), (), s32[]{:S(2)}) async-start(), calls=%async_computation.48 | async-start | bytes 8601600 | tf_op jit(solution)/shard_map/reduce_scatter | solution.py:308
  1538.0 410.7 %reduce-scatter.57.cloned.1.call-start = ((), (), s32[]{:S(2)}) async-start(), calls=%async_computation.47 | async-start | bytes 8601600 | tf_op jit(solution)/shard_map/reduce_scatter | solution.py:307
  1547.3 479.2 %reduce-scatter.55.cloned.1.call-start = ((), (), s32[]{:S(2)}) async-start(), calls=%async_computation.46 | async-start | bytes 8601600 | tf_op jit(solution)/shard_map/reduce_scatter | solution.py:307
  1556.9 501.3 %reduce-scatter.53.cloned.1.call-start = ((), (), s32[]{:S(2)}) async-start(), calls=%async_computation.45 | async-start | bytes 1474560 | tf_op jit(solution)/shard_map/reduce_scatter | solution.py:306
  1562.0 527.7 %reduce-scatter.51.cloned.1.call-start = ((), (), s32[]{:S(2)}) async-start(), calls=%async_computation.44 | async-start | bytes 1474560 | tf_op jit(solution)/shard_map/reduce_scatter | solution.py:306
  1566.2 550.3 %reduce-scatter.83.cloned.1.call-start = ((), (), s32[]{:S(2)}) async-start(), calls=%async_computation.66 | async-start | bytes 81920
  1588.1 562.6 %reduce-scatter.49.cloned.1.call-start = ((), (), s32[]{:S(2)}) async-start(), calls=%async_computation.43 | async-start | bytes 1966080 | tf_op jit(solution)/shard_map/reduce_scatter | solution.py:304
  1592.2 592.6 %reduce-scatter.47.cloned.1.call-start = ((), (), s32[]{:S(2)}) async-start(), calls=%async_computation.42 | async-start | bytes 1966080 | tf_op jit(solution)/shard_map/reduce_scatter | solution.py:304
  1596.6 660.2 %reduce-scatter.81.cloned.1.call-start = ((), (), s32[]{:S(2)}) async-start(), calls=%async_computation.65 | async-start | bytes 7077888 | tf_op jit(solution)/shard_map/reduce_scatter | solution.py:70
  (89 other events, 5633.1 us)
Sparse Core Ops, SparseCore 0:
  31.3 36.4 all-gather.28
  95.1 22.7 all-gather.30
  150.4 69.6 reduce-scatter.66
  384.9 69.7 reduce-scatter.68
  909.4 68.6 reduce-scatter.74
  996.0 36.5 all-gather.42
  1068.0 34.5 reduce-scatter.42
  1134.5 68.7 reduce-scatter.76
  1205.6 68.3 reduce-scatter.72
  1427.9 36.5 all-gather.46
  1498.7 34.5 reduce-scatter.44
  1536.4 22.9 reduce-scatter.84
  1562.5 74.9 reduce-scatter.64
  1640.3 74.9 reduce-scatter.62
  1718.1 74.9 reduce-scatter.60
  1795.9 74.9 reduce-scatter.58
  1873.7 74.9 reduce-scatter.56
  1951.6 74.9 reduce-scatter.54
  2029.4 28.6 reduce-scatter.52
  2060.9 28.6 reduce-scatter.50
  2092.4 24.0 reduce-scatter.82
  2119.5 31.1 reduce-scatter.48
  2153.7 31.1 reduce-scatter.46
  2187.0 69.7 reduce-scatter.80
Sparse Core Ops, SparseCore 1:
  153.3 46.0 all-gather.48
  236.8 36.3 all-gather.32
  275.5 45.0 all-gather.50
  322.4 46.0 all-gather.52
  471.1 36.3 all-gather.34
  534.7 22.7 all-gather.36
  589.7 68.6 reduce-scatter.70
  660.1 44.5 all-gather.56
  706.7 38.0 all-gather.38
  746.6 45.0 all-gather.54
  793.4 46.0 all-gather.58
  841.1 38.0 all-gather.40
  1276.8 36.5 all-gather.44
  1341.7 68.6 reduce-scatter.78
where the time goes:
time: 2300 us; the launch traced here: 2290 us
  waiting for transfers between devices  1610 us (70%)
  blocking collectives  260 us (11%)
  matrix products  220 us (10%)
  local copies, waits for them, and re-layouts  99 us (4%)
  other arithmetic  63.8 us (3%)
    reduce_scatter x8, waiting for transfers between devices, summed_rows(): lax.psum_scatter(make_term(jnp.int32(0), lax.axis_size('col') * rows), 'c...  519 us
    all_gather x8, waiting for transfers between devices, spread(): return lax.all_gather(values, 'col', axis=0, tiled=True)  249 us
    reduce_scatter x2, waiting for transfers between devices, per_device(): lax.psum_scatter(d_up_w, 'row', scatter_dimension=0, tiled=True)  152 us
    reduce_scatter x2, waiting for transfers between devices, per_device(): lax.psum_scatter(d_gate_w, 'row', scatter_dimension=0, tiled=True)  152 us
    psum x8, blocking collectives, feature_total(): return lax.psum(jnp.sum(values, axis=0), 'col')  115 us
    reduce_scatter x2, waiting for transfers between devices, per_device(): lax.psum_scatter(d_down, 'row', scatter_dimension=1, tiled=True)  107 us
    all_gather x2, waiting for transfers between devices, per_device(): lax.all_gather(down_weight[layer], 'row', axis=1, tiled=True)  75.7 us
    dot_general x10, matrix products, contract_last(): lax.dot_general(left, right, (((1,), (1,)), ((), ())), preferred_element_...  71.6 us
  transfers between devices with their start and end apart: 42, of which 38 were waited for; matrix products, arithmetic and copies ran while one was open for 8% of the time, Pallas kernels for 0%

commit v1 on v0

--- a/solution.py
+++ b/solution.py
@@ -63,7 +63,9 @@
 
 
 def spread(values):
-    return lax.all_gather(values, "col", axis=0, tiled=True)
+    return jnp.concatenate(
+        lax.all_to_all(jnp.stack([values] * lax.axis_size("col")), "col", 0, 0), axis=0
+    )
 
 
 def summed_rows(make_term, rows):

time: 2300 us -> 2440 us (1.061)
  blocking collectives: 260 us -> 482 us
  waiting for transfers between devices: 1610 us -> 1470 us
  local copies, waits for them, and re-layouts: 99 us -> 143 us
    reduce_scatter x8 -> x0, waiting for transfers between devices: 519 us -> none  [summed_rows(): lax.psum_scatter(make_term(jnp.int32(0), lax.axis_size('col') * rows), 'c...]
    unnamed x40, waiting for transfers between devices: 28 us -> 542 us
    all_to_all x0 -> x5, waiting for transfers between devices: none -> 260 us  [spread(): lax.all_to_all(jnp.stack([values] * lax.axis_size('col')), 'col', 0, 0)]
    all_gather x8 -> x0, waiting for transfers between devices: 249 us -> none  [spread(): return lax.all_gather(values, 'col', axis=0, tiled=True)]
    all_to_all x0 -> x3, blocking collectives: none -> 223 us  [spread(): lax.all_to_all(jnp.stack([values] * lax.axis_size('col')), 'col', 0, 0)]
    all_gather x2, waiting for transfers between devices: 66.4 us -> 0.03 us  [per_device(): lax.all_gather(up_weight[layer], 'row', axis=0, tiled=True)]
    all_gather x2, waiting for transfers between devices: 75.7 us -> 30.9 us  [per_device(): lax.all_gather(down_weight[layer], 'row', axis=1, tiled=True)]
    all_gather x2, waiting for transfers between devices: 38.1 us -> 0.03 us  [per_device(): lax.all_gather(gate_weight[layer], 'row', axis=0, tiled=True)]
  transfers between devices with their start and end apart: 42 -> 39, of which waited for: 38 -> 32; matrix products, arithmetic and copies ran while one was open for 8% -> 8% of each run, Pallas kernels for 0% -> 0%
where the time goes in v1:
time: 2440 us; the launch traced here: 2430 us
  waiting for transfers between devices  1470 us (60%)
  blocking collectives  482 us (20%)
  matrix products  217 us (9%)
  local copies, waits for them, and re-layouts  143 us (6%)
  other arithmetic  62.8 us (3%)
  starting transfers between devices  39.5 us (2%)
    unnamed x40, waiting for transfers between devices  542 us
    all_to_all x5, waiting for transfers between devices, spread(): lax.all_to_all(jnp.stack([values] * lax.axis_size('col')), 'col', 0, 0)  260 us
    all_to_all x3, blocking collectives, spread(): lax.all_to_all(jnp.stack([values] * lax.axis_size('col')), 'col', 0, 0)  223 us
    reduce_scatter x2, waiting for transfers between devices, per_device(): lax.psum_scatter(d_up_w, 'row', scatter_dimension=0, tiled=True)  152 us
    reduce_scatter x2, waiting for transfers between devices, per_device(): lax.psum_scatter(d_gate_w, 'row', scatter_dimension=0, tiled=True)  152 us
    psum x8, blocking collectives, feature_total(): return lax.psum(jnp.sum(values, axis=0), 'col')  114 us
    reduce_scatter x2, waiting for transfers between devices, per_device(): lax.psum_scatter(d_down, 'row', scatter_dimension=1, tiled=True)  107 us
    unnamed x190, local copies, waits for them, and re-layouts  84.6 us
  transfers between devices with their start and end apart: 39, of which 32 were waited for; matrix products, arithmetic and copies ran while one was open for 8% of the time, Pallas kernels for 0%

profile of v1, /device:TPU:0, one launch (start us, length us, event | category | flops | bytes accessed | tf_op | source)
XLA Modules:
  0.0 2429.7 jit_solution(7483413580730255076)
XLA Ops:
  59.8 48.2 %all-to-all-done = bf16[8,192,1024]{2,1,0:T(8,128)(2,1)} async-done(((bf16[8,192,1024]{2,1,0:T(8,128)(2,1)}), bf16[8,192,1024]{2,1,0:T(8,128)(2,1)}, u32[]{:S(2)}, u32[]{:S(2)}) %all-to-all-start) | async-done | bytes 3145760 | tf_op jit(solution)/shard_map/all_to_all | solution.py:67
  134.8 22.7 all-gather.21.cloned.1.call-done
  196.2 64.0 %reduce-scatter.67.cloned.1.call-done = f32[192,1024]{1,0:T(8,128)} async-done(((f32[1536,1024]{1,0:T(8,128)}), f32[192,1024]{1,0:T(8,128)}) %reduce-scatter.67.cloned.1.call-update) | async-done | bytes 786448
  288.9 68.5 %all-to-all-done.3 = bf16[8,192,1024]{2,1,0:T(8,128)(2,1)} async-done(((bf16[8,192,1024]{2,1,0:T(8,128)(2,1)}), bf16[8,192,1024]{2,1,0:T(8,128)(2,1)}, u32[]{:S(2)}, u32[]{:S(2)}) %all-to-all-start.3) | async-done | bytes 3145760 | tf_op jit(solution)/shard_map/all_to_all | solution.py:67
  393.6 68.9 %reduce-scatter.69.cloned.1.call-done = f32[192,1024]{1,0:T(8,128)} async-done(((f32[1536,1024]{1,0:T(8,128)}), f32[192,1024]{1,0:T(8,128)}) %reduce-scatter.69.cloned.1.call-update) | async-done | bytes 786448
  508.6 51.2 %all-to-all-done.4 = bf16[8,192,1024]{2,1,0:T(8,128)(2,1)} async-done(((bf16[8,192,1024]{2,1,0:T(8,128)(2,1)}), bf16[8,192,1024]{2,1,0:T(8,128)(2,1)}, u32[]{:S(2)}, u32[]{:S(2)}) %all-to-all-start.4) | async-done | bytes 3145760 | tf_op jit(solution)/shard_map/all_to_all | solution.py:67
  586.9 23.0 all-gather.23.cloned.1.call-done
  642.9 68.2 %reduce-scatter.71.cloned.1.call-done = f32[192,1024]{1,0:T(8,128)} async-done(((f32[1536,1024]{1,0:T(8,128)}), f32[192,1024]{1,0:T(8,128)}) %reduce-scatter.71.cloned.1.call-update) | async-done | bytes 786448
  734.2 70.8 %all-to-all-done.7 = bf16[8,192,1024]{2,1,0:T(8,128)(2,1)} async-done(((bf16[8,192,1024]{2,1,0:T(8,128)(2,1)}), bf16[8,192,1024]{2,1,0:T(8,128)(2,1)}, u32[]{:S(2)}, u32[]{:S(2)}) %all-to-all-start.7) | async-done | bytes 3145760 | tf_op jit(solution)/shard_map/all_to_all | solution.py:67
  830.7 30.9 %all-gather.35.cloned.1.call-done = bf16[1,1120,1536]{2,1,0:T(8,128)(2,1)} async-done(((bf16[1,1120,384]{2,1,0:T(8,128)(2,1)}), bf16[1,1120,1536]{2,1,0:T(8,128)(2,1)}) %all-gather.35.cloned.1.call-update) | async-done | bytes 3440656 | tf_op jit(solution)/shard_map/all_gather | solution.py:162
  861.7 21.4 all-to-all-done.8
  930.5 51.6 %reduce-scatter.75.cloned.1.call-done = f32[192,1024]{1,0:T(8,128)} async-done(((f32[1536,1024]{1,0:T(8,128)}), f32[192,1024]{1,0:T(8,128)}) %reduce-scatter.75.cloned.1.call-update) | async-done | bytes 786448
  998.5 54.2 %reduce-scatter.73.cloned.1.call-done = f32[192,1024]{1,0:T(8,128)} async-done(((f32[1536,1024]{1,0:T(8,128)}), f32[192,1024]{1,0:T(8,128)}) %reduce-scatter.73.cloned.1.call-update) | async-done | bytes 786448
  1058.8 74.1 %all_to_all.170 = bf16[8,192,1024]{2,1,0:T(8,128)(2,1)S(1)} all-to-all(bf16[8,192,1024]{2,1,0:T(8,128)(2,1)S(1)} %stack.75), channel_id=1, replica_groups=mesh['row'=4,'col'=8] {'col'}, dimensions={0} | all-to-all | bytes 6291456 | tf_op jit(solution)/shard_map/all_to_all | solution.py:67
  1172.4 30.2 %reduce-scatter.43.cloned.1.call-done = f32[512,128]{1,0:T(8,128)} async-done(((f32[512,1024]{1,0:T(8,128)}), f32[512,128]{1,0:T(8,128)}) %reduce-scatter.43.cloned.1.call-update) | async-done | bytes 262160 | tf_op jit(solution)/shard_map/reduce_scatter | solution.py:292
  1206.0 18.4 all_to_all.171
  1238.2 68.5 %reduce-scatter.77.cloned.1.call-done = f32[192,1024]{1,0:T(8,128)} async-done(((f32[1536,1024]{1,0:T(8,128)}), f32[192,1024]{1,0:T(8,128)}) %reduce-scatter.77.cloned.1.call-update) | async-done | bytes 786448
  1330.5 74.5 %all_to_all.172 = bf16[8,192,1024]{2,1,0:T(8,128)(2,1)S(1)} all-to-all(bf16[8,192,1024]{2,1,0:T(8,128)(2,1)S(1)} %stack.76), channel_id=1, replica_groups=mesh['row'=4,'col'=8] {'col'}, dimensions={0} | all-to-all | bytes 6291456 | tf_op jit(solution)/shard_map/all_to_all | solution.py:67
  1431.3 68.8 %reduce-scatter.79.cloned.1.call-done = f32[192,1024]{1,0:T(8,128)} async-done(((f32[1536,1024]{1,0:T(8,128)}), f32[192,1024]{1,0:T(8,128)}) %reduce-scatter.79.cloned.1.call-update) | async-done | bytes 786448
  1523.8 74.1 %all_to_all.173 = bf16[8,192,1024]{2,1,0:T(8,128)(2,1)S(1)} all-to-all(bf16[8,192,1024]{2,1,0:T(8,128)(2,1)S(1)} %stack.77), channel_id=1, replica_groups=mesh['row'=4,'col'=8] {'col'}, dimensions={0} | all-to-all | bytes 6291456 | tf_op jit(solution)/shard_map/all_to_all | solution.py:67
  1744.3 28.9 %reduce-scatter.65.cloned.1.call-done = f32[1120,384]{1,0:T(8,128)} async-done(((f32[1120,1536]{1,0:T(8,128)}), f32[1120,384]{1,0:T(8,128)}) %reduce-scatter.65.cloned.1.call-update) | async-done | bytes 1720336 | tf_op jit(solution)/shard_map/reduce_scatter | solution.py:311
  1773.1 77.8 %reduce-scatter.63.cloned.1.call-done = f32[1120,384]{1,0:T(8,128)} async-done(((f32[1120,1536]{1,0:T(8,128)}), f32[1120,384]{1,0:T(8,128)}) %reduce-scatter.63.cloned.1.call-update) | async-done | bytes 1720336 | tf_op jit(solution)/shard_map/reduce_scatter | solution.py:311
  1854.9 73.9 %reduce-scatter.61.cloned.1.call-done = f32[384,1120]{0,1:T(8,128)} async-done(((f32[1536,1120]{0,1:T(8,128)}), f32[384,1120]{0,1:T(8,128)}) %reduce-scatter.61.cloned.1.call-update) | async-done | bytes 1720336 | tf_op jit(solution)/shard_map/reduce_scatter | solution.py:310
  1928.8 77.8 %reduce-scatter.59.cloned.1.call-done = f32[384,1120]{0,1:T(8,128)} async-done(((f32[1536,1120]{0,1:T(8,128)}), f32[384,1120]{0,1:T(8,128)}) %reduce-scatter.59.cloned.1.call-update) | async-done | bytes 1720336 | tf_op jit(solution)/shard_map/reduce_scatter | solution.py:310
  2010.6 73.9 %reduce-scatter.57.cloned.1.call-done = f32[384,1120]{0,1:T(8,128)} async-done(((f32[1536,1120]{0,1:T(8,128)}), f32[384,1120]{0,1:T(8,128)}) %reduce-scatter.57.cloned.1.call-update) | async-done | bytes 1720336 | tf_op jit(solution)/shard_map/reduce_scatter | solution.py:309
  2084.4 77.8 %reduce-scatter.55.cloned.1.call-done = f32[384,1120]{0,1:T(8,128)} async-done(((f32[1536,1120]{0,1:T(8,128)}), f32[384,1120]{0,1:T(8,128)}) %reduce-scatter.55.cloned.1.call-update) | async-done | bytes 1720336 | tf_op jit(solution)/shard_map/reduce_scatter | solution.py:309
  2166.2 27.6 %reduce-scatter.53.cloned.1.call-done = f32[192,384]{1,0:T(8,128)} async-done(((f32[192,1536]{1,0:T(8,128)}), f32[192,384]{1,0:T(8,128)}) %reduce-scatter.53.cloned.1.call-update) | async-done | bytes 294928 | tf_op jit(solution)/shard_map/reduce_scatter | solution.py:308
  2193.9 31.5 %reduce-scatter.51.cloned.1.call-done = f32[192,384]{1,0:T(8,128)} async-done(((f32[192,1536]{1,0:T(8,128)}), f32[192,384]{1,0:T(8,128)}) %reduce-scatter.51.cloned.1.call-update) | async-done | bytes 294928 | tf_op jit(solution)/shard_map/reduce_scatter | solution.py:308
  2227.3 25.5 %reduce-scatter.83.cloned.1.call-done = f32[32,2]{1,0:T(8,128)} async-done(((f32[128,2]{1,0:T(8,128)}), f32[32,2]{1,0:T(8,128)}) %reduce-scatter.83.cloned.1.call-update) | async-done | bytes 272
  2254.2 32.8 %reduce-scatter.49.cloned.1.call-done = f32[384,256]{1,0:T(8,128)} async-done(((f32[1536,256]{1,0:T(8,128)}), f32[384,256]{1,0:T(8,128)}) %reduce-scatter.49.cloned.1.call-update) | async-done | bytes 393232 | tf_op jit(solution)/shard_map/reduce_scatter | solution.py:306
  2287.0 34.2 %reduce-scatter.47.cloned.1.call-done = f32[384,256]{1,0:T(8,128)} async-done(((f32[1536,256]{1,0:T(8,128)}), f32[384,256]{1,0:T(8,128)}) %reduce-scatter.47.cloned.1.call-update) | async-done | bytes 393232 | tf_op jit(solution)/shard_map/reduce_scatter | solution.py:306
  2323.2 69.9 %reduce-scatter.81.cloned.1.call-done = f32[192,1024]{1,0:T(8,128)} async-done(((f32[1536,1024]{1,0:T(8,128)}), f32[192,1024]{1,0:T(8,128)}) %reduce-scatter.81.cloned.1.call-update) | async-done | bytes 786448
  (448 shorter events, 728.4 us)
Async XLA Ops:
  31.9 76.1 %all-to-all-start = ((bf16[8,192,1024]{2,1,0:T(8,128)(2,1)}), bf16[8,192,1024]{2,1,0:T(8,128)(2,1)}, u32[]{:S(2)}, u32[]{:S(2)}) async-start(bf16[8,192,1024]{2,1,0:T(8,128)(2,1)} %stack.70), calls=%async_computation | async-start | bytes 6291456 | tf_op jit(solution)/shard_map/all_to_all | solution.py:67
  36.5 121.0 %all-gather.21.cloned.1.call-start = ((), (), s32[]{:S(2)}) async-start(), calls=%async_computation.38 | async-start | bytes 1179648 | tf_op jit(solution)/shard_map/all_gather | solution.py:172
  167.6 92.6 %reduce-scatter.67.cloned.1.call-start = ((), (), s32[]{:S(2)}) async-start(), calls=%async_computation.58 | async-start | bytes 7077888
  190.5 98.4 %all-gather.25.cloned.1.call-start = ((), (), s32[]{:S(2)}) async-start(), calls=%async_computation.52 | async-start | bytes 4300800 | tf_op jit(solution)/shard_map/all_gather | solution.py:160
  193.3 172.9 %all-gather.27.cloned.1.call-start = ((), (), s32[]{:S(2)}) async-start(), calls=%async_computation.53 | async-start | bytes 4300800 | tf_op jit(solution)/shard_map/all_gather | solution.py:161
  281.4 76.0 %all-to-all-start.3 = ((bf16[8,192,1024]{2,1,0:T(8,128)(2,1)}), bf16[8,192,1024]{2,1,0:T(8,128)(2,1)}, u32[]{:S(2)}, u32[]{:S(2)}) async-start(bf16[8,192,1024]{2,1,0:T(8,128)(2,1)} %stack.71), calls=%async_computation.3 | async-start | bytes 6291456 | tf_op jit(solution)/shard_map/all_to_all | solution.py:67
  285.9 91.5 %all-gather.29.cloned.1.call-start = ((), (), s32[]{:S(2)}) async-start(), calls=%async_computation.54 | async-start | bytes 4300800 | tf_op jit(solution)/shard_map/all_gather | solution.py:162
  288.8 173.7 %reduce-scatter.69.cloned.1.call-start = ((), (), s32[]{:S(2)}) async-start(), calls=%async_computation.59 | async-start | bytes 7077888
  483.8 76.0 %all-to-all-start.4 = ((bf16[8,192,1024]{2,1,0:T(8,128)(2,1)}), bf16[8,192,1024]{2,1,0:T(8,128)(2,1)}, u32[]{:S(2)}, u32[]{:S(2)}) async-start(bf16[8,192,1024]{2,1,0:T(8,128)(2,1)} %stack.72), calls=%async_computation.4 | async-start | bytes 6291456 | tf_op jit(solution)/shard_map/all_to_all | solution.py:67
  488.3 121.7 %all-gather.23.cloned.1.call-start = ((), (), s32[]{:S(2)}) async-start(), calls=%async_computation.39 | async-start | bytes 1179648 | tf_op jit(solution)/shard_map/all_gather | solution.py:172
  619.3 91.7 %reduce-scatter.71.cloned.1.call-start = ((), (), s32[]{:S(2)}) async-start(), calls=%async_computation.60 | async-start | bytes 7077888
  642.1 170.4 %all-gather.33.cloned.1.call-start = ((), (), s32[]{:S(2)}) async-start(), calls=%async_computation.56 | async-start | bytes 4300800 | tf_op jit(solution)/shard_map/all_gather | solution.py:161
  728.9 76.1 %all-to-all-start.7 = ((bf16[8,192,1024]{2,1,0:T(8,128)(2,1)}), bf16[8,192,1024]{2,1,0:T(8,128)(2,1)}, u32[]{:S(2)}, u32[]{:S(2)}) async-start(bf16[8,192,1024]{2,1,0:T(8,128)(2,1)} %stack.73), calls=%async_computation.7 | async-start | bytes 6291456 | tf_op jit(solution)/shard_map/all_to_all | solution.py:67
  733.5 87.9 %all-gather.31.cloned.1.call-start = ((), (), s32[]{:S(2)}) async-start(), calls=%async_computation.55 | async-start | bytes 4300800 | tf_op jit(solution)/shard_map/all_gather | solution.py:160
  812.3 169.8 %reduce-scatter.75.cloned.1.call-start = ((), (), s32[]{:S(2)}) async-start(), calls=%async_computation.62 | async-start | bytes 7077888
  913.2 139.6 %reduce-scatter.73.cloned.1.call-start = ((), (), s32[]{:S(2)}) async-start(), calls=%async_computation.61 | async-start | bytes 7077888
  1167.7 139.0 %reduce-scatter.77.cloned.1.call-start = ((), (), s32[]{:S(2)}) async-start(), calls=%async_computation.63 | async-start | bytes 7077888
  1238.1 261.9 %reduce-scatter.79.cloned.1.call-start = ((), (), s32[]{:S(2)}) async-start(), calls=%async_computation.64 | async-start | bytes 7077888
  1604.6 96.6 %reduce-scatter.45.cloned.1.call-start = ((), (), s32[]{:S(2)}) async-start(), calls=%async_computation.41 | async-start | bytes 2359296 | tf_op jit(solution)/shard_map/reduce_scatter | solution.py:292
  1634.4 109.0 %reduce-scatter.85.cloned.1.call-start = ((), (), s32[]{:S(2)}) async-start(), calls=%async_computation.67 | async-start | bytes 81920
  1636.4 136.7 %reduce-scatter.65.cloned.1.call-start = ((), (), s32[]{:S(2)}) async-start(), calls=%async_computation.51 | async-start | bytes 8601600 | tf_op jit(solution)/shard_map/reduce_scatter | solution.py:311
  1645.6 205.3 %reduce-scatter.63.cloned.1.call-start = ((), (), s32[]{:S(2)}) async-start(), calls=%async_computation.50 | async-start | bytes 8601600 | tf_op jit(solution)/shard_map/reduce_scatter | solution.py:311
  1654.9 273.9 %reduce-scatter.61.cloned.1.call-start = ((), (), s32[]{:S(2)}) async-start(), calls=%async_computation.49 | async-start | bytes 8601600 | tf_op jit(solution)/shard_map/reduce_scatter | solution.py:310
  1664.7 341.9 %reduce-scatter.59.cloned.1.call-start = ((), (), s32[]{:S(2)}) async-start(), calls=%async_computation.48 | async-start | bytes 8601600 | tf_op jit(solution)/shard_map/reduce_scatter | solution.py:310
  1674.0 410.5 %reduce-scatter.57.cloned.1.call-start = ((), (), s32[]{:S(2)}) async-start(), calls=%async_computation.47 | async-start | bytes 8601600 | tf_op jit(solution)/shard_map/reduce_scatter | solution.py:309
  1683.3 479.0 %reduce-scatter.55.cloned.1.call-start = ((), (), s32[]{:S(2)}) async-start(), calls=%async_computation.46 | async-start | bytes 8601600 | tf_op jit(solution)/shard_map/reduce_scatter | solution.py:309
  1692.7 501.1 %reduce-scatter.53.cloned.1.call-start = ((), (), s32[]{:S(2)}) async-start(), calls=%async_computation.45 | async-start | bytes 1474560 | tf_op jit(solution)/shard_map/reduce_scatter | solution.py:308
  1696.0 529.3 %reduce-scatter.51.cloned.1.call-start = ((), (), s32[]{:S(2)}) async-start(), calls=%async_computation.44 | async-start | bytes 1474560 | tf_op jit(solution)/shard_map/reduce_scatter | solution.py:308
  1700.4 552.4 %reduce-scatter.83.cloned.1.call-start = ((), (), s32[]{:S(2)}) async-start(), calls=%async_computation.66 | async-start | bytes 81920
  1722.2 564.8 %reduce-scatter.49.cloned.1.call-start = ((), (), s32[]{:S(2)}) async-start(), calls=%async_computation.43 | async-start | bytes 1966080 | tf_op jit(solution)/shard_map/reduce_scatter | solution.py:306
  1726.5 594.6 %reduce-scatter.47.cloned.1.call-start = ((), (), s32[]{:S(2)}) async-start(), calls=%async_computation.42 | async-start | bytes 1966080 | tf_op jit(solution)/shard_map/reduce_scatter | solution.py:306
  1731.1 662.0 %reduce-scatter.81.cloned.1.call-start = ((), (), s32[]{:S(2)}) async-start(), calls=%async_computation.65 | async-start | bytes 7077888
  (89 other events, 4067.2 us)
Sparse Core Ops, SparseCore 0:
  134.6 22.7 all-gather.20
  190.6 69.5 reduce-scatter.66
  393.7 68.7 reduce-scatter.68
  587.0 22.8 all-gather.22
  642.3 68.7 reduce-scatter.70
  913.3 68.7 reduce-scatter.74
  984.4 68.3 reduce-scatter.72
  1167.8 34.7 reduce-scatter.42
  1238.2 68.4 reduce-scatter.76
  1431.4 68.6 reduce-scatter.78
  1634.5 34.8 reduce-scatter.44
  1672.6 22.4 reduce-scatter.84
  1698.1 74.9 reduce-scatter.64
  1776.0 74.9 reduce-scatter.62
  1853.8 74.9 reduce-scatter.60
  1931.6 74.9 reduce-scatter.58
  2009.4 74.9 reduce-scatter.56
  2087.3 74.9 reduce-scatter.54
  2165.1 28.6 reduce-scatter.52
  2196.6 28.6 reduce-scatter.50
  2228.7 24.0 reduce-scatter.82
  2255.8 31.1 reduce-scatter.48
  2290.0 31.1 reduce-scatter.46
  2323.3 69.7 reduce-scatter.80
Sparse Core Ops, SparseCore 1:
  193.4 45.9 all-gather.24
  241.0 46.0 all-gather.26
  288.9 47.5 all-gather.28
  644.7 45.0 all-gather.32
  736.7 47.5 all-gather.30
  814.1 47.5 all-gather.34
